TPU v7x, 32 devices: a whole 2x2x4 slice. The times are simulated.
32 devices in a mesh: groups: 2 (over y), ctx: 4 (over z), tp: 4 (over x, core).
Axes of the slice: x: 2, y: 2, z: 4, core: 2. Of those that a mesh axis runs over, the one named last changes fastest.
Arguments:
- q_nope: bfloat16 [512, 16384], P(('groups', 'ctx'), 'tp'), parts along dimension 0, may hold values from -6 to 6
- q_rope: bfloat16 [512, 8192], P(('groups', 'ctx'), 'tp'), parts along dimension 0, may hold values from -6 to 6
- c_kv: bfloat16 [512, 512], P(('groups', 'ctx')), parts along dimension 0, may hold values from -6 to 46.4
- k_rope: bfloat16 [512, 64], P(('groups', 'ctx')), parts along dimension 0, may hold values from -6 to 6
- positions: int32 [512], P(('groups', 'ctx')), parts along dimension 0, may hold values from 0 to 255, as said below
- w_uk: bfloat16 [128, 128, 512], P('tp', 'ctx'), may hold values from -0.5 to 0.5
- w_uv: bfloat16 [128, 512, 128], P('tp', 'ctx'), may hold values from -0.25 to 0.25
- w_out: bfloat16 [16384, 7168], P('tp', 'ctx'), may hold values from -0.125 to 0.125
Outputs:
- attn_proj: bfloat16 [512, 7168], P(('groups', 'tp'), 'ctx'), parts along dimension 0
There are 2 independent parts, one for each index of `groups`. A program takes and returns all parts, laid end to end along the dimension named above; an argument that names none is the same for every part. Nothing has to cross between parts.
Inputs may be any that keep to these rules, and one draw needn't show every extreme that they name: The positions are the 256 integers 0 to 255, each once; every aligned block of 32 rows holds consecutive ascending positions.
All inputs are finite; a program needn't handle non-finite values.
Results may differ from a plain program's by a relative error of at most 0.015.
Values may be sent and summed in bfloat16 or wider, within the bound.
A program may use at most 64 MiB of HBM per device.

v0:
```python
import jax
import jax.numpy as jnp
from jax import lax
from jax.sharding import PartitionSpec as P


def rotate(values, position):
    half_dim = values.shape[-1] // 2
    freqs = 10000.0 ** (-jnp.arange(half_dim, dtype=jnp.float32) / half_dim)
    angles = position.astype(jnp.float32)[..., None] * freqs
    cosine = jnp.cos(angles)
    sine = jnp.sin(angles)
    first_half = values[..., :half_dim].astype(jnp.float32)
    second_half = values[..., half_dim:].astype(jnp.float32)
    return jnp.concatenate(
        [first_half * cosine - second_half * sine, second_half * cosine + first_half * sine],
        axis=-1,
    )


def on_device(q_nope, q_rope, c_kv, k_rope, positions, w_uk, w_uv, w_out):
    tok_count = q_nope.shape[0]
    head_count = w_uk.shape[0]
    latent = c_kv.shape[1]
    up_key, up_value = (
        lax.all_gather(w_uk, "ctx", axis=1, tiled=True),
        lax.all_gather(w_uv, "ctx", axis=1, tiled=True),
    )
    nope_dim = up_key.shape[1]
    rope_dim = k_rope.shape[1]
    softmax_scale = (nope_dim + rope_dim) ** (-0.5)
    q_parts = q_nope.reshape(tok_count, head_count, nope_dim)
    q_lat = jnp.einsum("thn,hnl->thl", q_parts, up_key, preferred_element_type=jnp.float32).astype(
        jnp.bfloat16
    )
    q_rot = rotate(q_rope.reshape(tok_count, head_count, rope_dim), positions[:, None]).astype(
        jnp.bfloat16
    )
    k_rot = rotate(k_rope, positions).astype(jnp.bfloat16)
    key_rows = jnp.concatenate([c_kv, k_rot], axis=1)
    queries = jnp.concatenate([q_lat, q_rot], axis=2).reshape(
        tok_count * head_count, latent + rope_dim
    )
    query_pos = jnp.repeat(positions, head_count)
    row_total = tok_count * head_count
    key_part = lax.all_gather(key_rows, "ctx", axis=0, tiled=True)
    key_pos = lax.all_gather(positions, "ctx", axis=0, tiled=True)
    run_max = jnp.full((row_total,), -1e30, jnp.float32)
    scores = (
        jnp.einsum("rk,sk->rs", queries, key_part, preferred_element_type=jnp.float32)
        * softmax_scale
    )
    visible = key_pos[None, :] <= query_pos[:, None]
    new_max = jnp.maximum(run_max, jnp.max(jnp.where(visible, scores, -1e30), axis=1))
    weights = jnp.where(visible, jnp.exp(scores - new_max[:, None]), 0.0)
    new_sum = jnp.sum(weights, axis=1)
    added = jnp.dot(
        weights.astype(jnp.bfloat16), key_part[:, :latent], preferred_element_type=jnp.float32
    )
    o_lat = (added / new_sum[:, None]).astype(jnp.bfloat16).reshape(tok_count, head_count, latent)
    head_out = jnp.einsum("thl,hlv->thv", o_lat, up_value, preferred_element_type=jnp.float32)
    rows_out = head_out.astype(jnp.bfloat16).reshape(tok_count, -1)
    partial_value = jnp.dot(
        lax.all_gather(rows_out, "ctx", axis=0, tiled=True),
        w_out,
        preferred_element_type=jnp.float32,
    )
    summed = lax.psum_scatter(
        partial_value.astype(jnp.bfloat16), "tp", scatter_dimension=0, tiled=True
    )
    return summed


def solution(mesh):
    in_specs = (
        P(("groups", "ctx"), "tp"),
        P(("groups", "ctx"), "tp"),
        P(("groups", "ctx"), None),
        P(("groups", "ctx"), None),
        P(("groups", "ctx")),
        P("tp", "ctx", None),
        P("tp", "ctx", None),
        P("tp", "ctx"),
    )
    out_specs = P(("groups", "tp"), "ctx")
    return jax.shard_map(
        on_device, mesh=mesh, in_specs=in_specs, out_specs=out_specs, check_vma=False
    )
```

profile of v0, /device:TPU:0, one launch (start us, length us, event | category | flops | bytes accessed | tf_op | source)
XLA Modules:
  0.0 268.4 jit_solution(3727803021012420115)
XLA Ops:
  6.6 0.7 all-gather.4.cloned.1.call-update
  7.3 0.7 all-gather.6.cloned.1.call-update
  8.1 0.5 reshape.91
  8.8 0.6 dynamic-slice
  10.1 0.2 dynamic-update-slice
  10.3 9.9 %all-reduce = s32[256]{0:T(256)S(1)} all-reduce(s32[256]{0:T(256)S(1)} %dynamic-update-slice), channel_id=1, replica_groups=mesh['groups'=2,'ctx'=4,'tp'=4] {'ctx'}, use_global_device_ids=true, to_apply=%add | all-reduce | flops 256 | bytes 2048
  20.2 0.2 fusion.24
  20.5 17.4 %all_gather.17 = bf16[256,576]{1,0:T(8,128)(2,1)S(1)} all-gather(bf16[64,576]{1,0:T(8,128)(2,1)S(1)} %pad_maximum_fusion.1), channel_id=1, replica_groups=mesh['groups'=2,'ctx'=4,'tp'=4] {'ctx'}, dimensions={0}, use_global_device_ids=true | all-gather | bytes 368640 | tf_op jit(solution)/shard_map/all_gather | solution.py:46
  37.9 0.2 fusion.28
  38.2 0.5 fusion.12
  38.6 58.2 %all-gather.4.cloned.1.call-done = bf16[32,128,512]{2,1,0:T(8,128)(2,1)} async-done(((bf16[32,32,512]{2,1,0:T(8,128)(2,1)}), bf16[32,128,512]{2,1,0:T(8,128)(2,1)}) %all-gather.4.cloned.1.call-update) | async-done | bytes 4194320 | tf_op jit(solution)/shard_map/all_gather | solution.py:26
  96.8 2.9 %convert_bitcast_fusion = bf16[64,32,512]{2,0,1:T(8,128)(2,1)S(1)} fusion(bf16[32,128,512]{2,1,0:T(8,128)(2,1)} %all-gather.4.cloned.1.call-done, bf16[64,4096]{1,0:T(8,128)(2,1)S(1)} %copy-done), kind=kOutput, calls=%fused_computation.9 | convolution fusion | flops 269484032 | bytes 6815744 | tf_op jit(solution)/shard_map/thn,hnl->thl/dot_general | solution.py:33
  99.7 0.5 pad_maximum_fusion
  100.2 1.5 copy.14
  101.7 1.1 fusion
  102.8 0.5 fusion.3
  103.3 0.9 divide_convert_fusion
  104.2 74.0 %all-gather.6.cloned.1.call-done = bf16[32,512,128]{2,1,0:T(8,128)(2,1)} async-done(((bf16[32,128,128]{2,1,0:T(8,128)(2,1)}), bf16[32,512,128]{2,1,0:T(8,128)(2,1)}) %all-gather.6.cloned.1.call-update) | async-done | bytes 4194320 | tf_op jit(solution)/shard_map/all_gather | solution.py:27
  178.1 4.8 %fusion.8 = bf16[32,8,8,128]{3,2,1,0:T(8,128)(2,1)S(1)} fusion(bf16[32,512,128]{2,1,0:T(8,128)(2,1)} %all-gather.6.cloned.1.call-done, bf16[64,32,512]{2,1,0:T(8,128)(2,1)S(1)} %bitcast.25), kind=kOutput, calls=%fused_computation.17 | convolution fusion | flops 268697600 | bytes 6815744 | tf_op jit(solution)/shard_map/thl,hlv->thv/dot_general | solution.py:61
  183.0 0.9 copy.36
  183.9 0.2 reduce-scatter.2.cloned.1.call-start
  184.2 44.1 %all-gather.8.cloned.1.call-done = bf16[256,4096]{1,0:T(8,128)(2,1)} async-done(((bf16[64,4096]{1,0:T(8,128)(2,1)}), bf16[256,4096]{1,0:T(8,128)(2,1)}) %all-gather.8.cloned.1.call-update) | async-done | bytes 2097168 | tf_op jit(solution)/shard_map/all_gather | solution.py:64
  228.2 10.7 %convolution_convert_fusion = bf16[256,1792]{1,0:T(8,128)(2,1)} fusion(bf16[256,4096]{1,0:T(8,128)(2,1)} %all-gather.8.cloned.1.call-done, bf16[4096,1792]{1,0:T(8,128)(2,1)} %param.15), kind=kOutput, calls=%fused_computation.5 | convolution fusion | flops 3758555136 | bytes 17694720 | tf_op jit(solution)/shard_map/dot_general | solution.py:63
  239.0 22.9 %reduce-scatter.2.cloned.1.call-done = bf16[64,1792]{1,0:T(8,128)(2,1)} async-done(((bf16[256,1792]{1,0:T(8,128)(2,1)}), bf16[64,1792]{1,0:T(8,128)(2,1)}) %reduce-scatter.2.cloned.1.call-update) | async-done | bytes 229392 | tf_op jit(solution)/shard_map/reduce_scatter | solution.py:68
  (24 shorter events, 0.4 us)
Async XLA Ops:
  6.5 90.3 %copy-start = (bf16[64,4096]{1,0:T(8,128)(2,1)S(1)}, bf16[64,4096]{1,0:T(8,128)(2,1)}, u32[]{:S(2)}) copy-start(bf16[64,4096]{1,0:T(8,128)(2,1)} %param.8) | copy-start | bytes 1572868
  6.5 2.3 copy-start.5
  6.5 1.6 copy-start.4
  6.5 1.6 copy-start.1
  6.5 13.7 %copy-start.3 = (bf16[64,64]{1,0:T(8,128)(2,1)S(1)}, bf16[64,64]{1,0:T(8,128)(2,1)}, u32[]{:S(2)}) copy-start(bf16[64,64]{1,0:T(8,128)(2,1)} %param.11) | copy-start | bytes 24580
  6.5 13.9 %copy-start.2 = (bf16[64,512]{1,0:T(8,128)(2,1)S(1)}, bf16[64,512]{1,0:T(8,128)(2,1)}, u32[]{:S(2)}) copy-start(bf16[64,512]{1,0:T(8,128)(2,1)} %param.10) | copy-start | bytes 196612
  6.6 90.2 %all-gather.4.cloned.1.call-start = ((), (), s32[]{:S(2)}) async-start(), calls=%async_computation.1 | async-start | bytes 5242880 | tf_op jit(solution)/shard_map/all_gather | solution.py:26
  7.3 170.9 %all-gather.6.cloned.1.call-start = ((), (), s32[]{:S(2)}) async-start(), calls=%async_computation.2 | async-start | bytes 5242880 | tf_op jit(solution)/shard_map/all_gather | solution.py:27
  8.0 220.2 %all-gather.8.cloned.1.call-start = ((), (), s32[]{:S(2)}) async-start(), calls=%async_computation.3 | async-start | bytes 2621440 | tf_op jit(solution)/shard_map/all_gather | solution.py:64
  183.9 78.0 %reduce-scatter.2.cloned.1.call-start = ((), (), s32[]{:S(2)}) async-start(), calls=%async_computation.4 | async-start | bytes 1146880 | tf_op jit(solution)/shard_map/reduce_scatter | solution.py:68
Sparse Core Ops, SparseCore 0:
  8.9 87.8 all-gather.3
  98.4 79.7 all-gather.5
  184.0 44.1 all-gather.7
  239.1 22.7 reduce-scatter.1
where the time goes:
time: 269 us; the launch traced here: 268 us
  waiting for transfers between devices  201 us (75%)
  blocking collectives  27.3 us (10%)
  matrix products  20.4 us (8%)
  between operations  13.9 us (5%)
  local copies, waits for them, and re-layouts  4.14 us (2%)
    all_gather x1, waiting for transfers between devices, on_device(): lax.all_gather(w_uv, 'ctx', axis=1, tiled=True)  74 us
    all_gather x1, waiting for transfers between devices, on_device(): lax.all_gather(w_uk, 'ctx', axis=1, tiled=True)  58.2 us
    all_gather x1, waiting for transfers between devices, on_device(): lax.all_gather(rows_out, 'ctx', axis=0, tiled=True)  44.1 us
    reduce_scatter x1, waiting for transfers between devices, on_device(): lax.psum_scatter(partial_value.astype(jnp.bfloat16), 'tp', scatter_dimens...  22.9 us
    all_gather x1, blocking collectives, on_device(): key_part = lax.all_gather(key_rows, 'ctx', axis=0, tiled=True)  17.4 us
    dot_general x1, matrix products, on_device(): jnp.dot(lax.all_gather(rows_out, 'ctx', axis=0, tiled=True), w_out, prefe...  10.7 us
    unnamed x1, blocking collectives  9.92 us
  transfers between devices with their start and end apart: 4, of which 4 were waited for; matrix products, arithmetic and copies ran while one was open for 4% of the time, Pallas kernels for 0%

commit v1 on v0

--- a/solution.py
+++ b/solution.py
@@ -1,7 +1,15 @@
+import functools
+
 import jax
 import jax.numpy as jnp
 from jax import lax
+from jax.experimental import pallas as pl
+from jax.experimental.pallas import tpu as pltpu
 from jax.sharding import PartitionSpec as P
+
+F32 = jnp.float32
+BF16 = jnp.bfloat16
+MESH = pl.DeviceIdType.MESH
 
 
 def rotate(values, position):
@@ -18,7 +26,313 @@
     )
 
 
-def on_device(q_nope, q_rope, c_kv, k_rope, positions, w_uk, w_uv, w_out):
+def rotate_flat(values, position, rope_dim):
+    half_dim = rope_dim // 2
+    copies = values.shape[1] // half_dim
+    freqs = 10000.0 ** (-jnp.arange(half_dim, dtype=jnp.float32) / half_dim)
+    angles = position.astype(jnp.float32)[:, None] * freqs
+    cosine = jnp.tile(jnp.cos(angles), (1, copies))
+    sine = jnp.tile(jnp.sin(angles), (1, copies))
+    wide = values.astype(jnp.float32)
+    lane = lax.broadcasted_iota(jnp.int32, wide.shape, 1)
+    low = lax.rem(lane, rope_dim) < half_dim
+    other = jnp.where(low, -jnp.roll(wide, -half_dim, axis=1), jnp.roll(wide, half_dim, axis=1))
+    return wide * cosine + other * sine
+
+
+def mega(sz, qn_in, qr_in, kv_in, wuk_in, wuv_in, wout_in, out_ref,
+         qn, qr, kv, wuk, wuv, wout, krot, ho, acc, part, got,
+         s1, r1, sy, ry, s_right, s_left, r_ag, s_rs, r_rs, loc, loc_out):
+    n, groups, tps, nch = sz["n"], sz["g"], sz["t"], sz["nch"]
+    tok, hpc, nope, rope, lat, vdim = (sz[k] for k in ("tok", "hpc", "nope", "rope", "lat", "vdim"))
+    scale = (nope + rope) ** (-0.5)
+    hc = hpc // nch
+    hg = hc // groups
+    c = lax.axis_index("ctx")
+    g = lax.axis_index("groups")
+    t = lax.axis_index("tp")
+    nsl = nope // n
+    lsl = lat // n
+
+    barrier = pltpu.get_barrier_semaphore()
+    for axis, me, count in (("ctx", c, n), ("groups", g, groups), ("tp", t, tps)):
+        for d in range(1, count):
+            pl.semaphore_signal(barrier, inc=1, device_id={axis: lax.rem(me + d, count)}, device_id_type=MESH)
+    pl.semaphore_wait(barrier, (n - 1) + (groups - 1) + (tps - 1))
+
+    def al(x, m):
+        return pl.multiple_of(x, m)
+
+    my_rows = pl.ds(al(c * tok, tok), tok)
+
+    def rows_of(s):
+        return pl.ds(al(s * tok, tok), tok)
+
+    def piece(kind, i, j, s, gg):
+        if kind == 0:
+            return kv_in, kv.at[rows_of(s), :]
+        if kind == 1:
+            w = hc * nope
+            return (qn_in.at[:, pl.ds(al(j * (hpc * nope) + i * w, w), w)],
+                    qn.at[rows_of(s), pl.ds(i * w, w)])
+        if kind == 2:
+            w = hc * rope
+            return (qr_in.at[:, pl.ds(al(j * (hpc * rope) + i * w, w), w)],
+                    qr.at[rows_of(s), pl.ds(i * w, w)])
+        if gg is None:
+            src_h, dst_h = pl.ds(j * hpc + i * hc, hc), pl.ds(i * hc, hc)
+        else:
+            src_h, dst_h = pl.ds(j * hpc + i * hc + gg * hg, hg), pl.ds(i * hc + gg * hg, hg)
+        if kind == 3:
+            return wuk_in.at[src_h], wuk.at[dst_h, pl.ds(al(s * nsl, nsl), nsl), :]
+        return wuv_in.at[src_h], wuv.at[dst_h, pl.ds(al(s * lsl, lsl), lsl), :]
+
+    def copy1(kind, i, d, sending):
+        if sending:
+            j = lax.rem(c + d, n)
+            src, dst = piece(kind, i, j, c, g)
+        else:
+            j = lax.rem(c + n - d, n)
+            src, dst = piece(kind, i, c, j, g)
+        return pltpu.make_async_remote_copy(
+            src_ref=src, dst_ref=dst, send_sem=s1.at[kind, i, d - 1], recv_sem=r1.at[kind, i, d - 1],
+            device_id={"ctx": j}, device_id_type=MESH)
+
+    def local(kind, i):
+        src, dst = piece(kind, i, c, c, None)
+        return pltpu.make_async_copy(src, dst, loc.at[kind, i])
+
+    def kinds(i):
+        return (0, 1, 2, 3, 4) if i == 0 else (1, 2, 3, 4)
+
+    for i in range(nch):
+        for kind in (3, 4, 0, 1, 2):
+            if kind in kinds(i):
+                for d in range(n - 1, 0, -1):
+                    copy1(kind, i, d, True).start()
+    for i in range(nch):
+        for kind in kinds(i):
+            local(kind, i).start()
+    wout_copy = pltpu.make_async_copy(wout_in, wout, loc_out)
+    wout_copy.start()
+
+    def copy_y(kind, i, e, d, sending):
+        s = lax.rem(c + n - d, n)
+        owner = g if sending else lax.rem(g + groups - e, groups)
+        _, dst = piece(kind, i, c, s, owner)
+        to = lax.rem(g + e, groups) if sending else owner
+        return pltpu.make_async_remote_copy(
+            src_ref=dst, dst_ref=dst, send_sem=sy.at[kind - 3, i, e - 1, d - 1],
+            recv_sem=ry.at[kind - 3, i, e - 1, d - 1],
+            device_id={"groups": to}, device_id_type=MESH)
+
+    def forward_weights(i):
+        for kind in (3, 4):
+            for d in range(1, n):
+                copy1(kind, i, d, False).wait_recv()
+                for e in range(1, groups):
+                    copy_y(kind, i, e, d, True).start()
+
+    def ag_ref(i, b):
+        return ho.at[b, i]
+
+    def ag_copy(i, b, right):
+        ref = ag_ref(i, b)
+        return pltpu.make_async_remote_copy(
+            src_ref=ref, dst_ref=ref, send_sem=(s_right if right else s_left).at[i, b],
+            recv_sem=r_ag.at[i, b],
+            device_id={"ctx": c + 1 if right else c - 1}, device_id_type=MESH)
+
+    def attend(i):
+        blk = kv[:, lat:lat + 2 * rope].astype(F32)
+        lane = lax.broadcasted_iota(jnp.int32, blk.shape, 1)
+        pos_col = jnp.sum(jnp.where(lane == rope, blk * 256.0, jnp.where(lane == rope + 1, blk, 0.0)),
+                          axis=1, keepdims=True)
+        blk_t = blk.T
+        pos_row = blk_t[rope:rope + 1, :] * 256.0 + blk_t[rope + 1:rope + 2, :]
+        hidden = pos_row > pos_col
+        even = jnp.where(lane < rope, blk, 0.0)
+        krot[0] = even.astype(BF16)
+        krot[1] = pltpu.roll(even, rope, 1).astype(BF16)
+        nt = (((1,), (1,)), ((), ()))
+
+        def pair(p, carry):
+            qrp = qr[:, pl.ds(al((i * (hc // 2) + p) * 2 * rope, 2 * rope), 2 * rope)]
+            for k in range(2):
+                hl = 2 * p + k
+                h = i * hc + hl
+                q = qn[:, pl.ds(al(h * nope, nope), nope)]
+                ql = jnp.dot(q, wuk[h], preferred_element_type=F32).astype(BF16)
+                sc = lax.dot_general(ql, kv[:, :lat], nt, preferred_element_type=F32)
+                sc = (sc + lax.dot_general(qrp, krot[k], nt, preferred_element_type=F32)) * scale
+                sc = jnp.where(hidden, -1e30, sc)
+                w = jnp.exp(sc - jnp.max(sc, axis=1, keepdims=True))
+                total = jnp.sum(w, axis=1, keepdims=True)
+                o = jnp.dot(w.astype(BF16), kv[:, :lat], preferred_element_type=F32)
+                o = (o / total).astype(BF16)
+                ho[c, i, :, pl.ds(al(hl * vdim, vdim), vdim)] = jnp.dot(
+                    o, wuv[h], preferred_element_type=F32).astype(BF16)
+            return carry
+
+        lax.fori_loop(0, hc // 2, pair, 0)
+
+    for i in range(nch):
+        if i == 0:
+            forward_weights(0)
+        for kind in (0, 1, 2):
+            if kind in kinds(i):
+                for d in range(1, n):
+                    copy1(kind, i, d, False).wait_recv()
+        for kind in kinds(i):
+            local(kind, i).wait()
+        for kind in (3, 4):
+            for e in range(1, groups):
+                for d in range(1, n):
+                    copy_y(kind, i, e, d, False).wait_recv()
+        if i + 1 < nch:
+            forward_weights(i + 1)
+        attend(i)
+
+        @pl.when(c + 1 < n)
+        def _():
+            ag_copy(i, c, True).start()
+
+        @pl.when(c > 0)
+        def _():
+            ag_copy(i, c, False).start()
+
+    cols = acc.shape[1]
+    tile = sz["tile"]
+    kdim = hc * vdim
+
+    def project(i, b, first):
+        rows = pl.ds(al(b * (hpc * vdim) + i * kdim, kdim), kdim)
+
+        def step(j, carry):
+            at = pl.ds(al(j * tile, tile), tile)
+            value = jnp.dot(ho[b, i], wout[rows, at], preferred_element_type=F32)
+            acc[:, at] = value if first else acc[:, at] + value
+            return carry
+
+        lax.fori_loop(0, cols // tile, step, 0)
+
+    wout_copy.wait()
+    for i in range(nch):
+        project(i, c, i == 0)
+    for d in range(1, n):
+        for i in range(nch):
+            @pl.when(c - d >= 0)
+            def _():
+                b = c - d
+                ag_copy(i, b, True).wait_recv()
+
+                @pl.when(c + 1 < n)
+                def _():
+                    ag_copy(i, b, True).start()
+
+            @pl.when(c + d < n)
+            def _():
+                b = c + d
+                ag_copy(i, b, False).wait_recv()
+
+                @pl.when(c > 0)
+                def _():
+                    ag_copy(i, b, False).start()
+
+            @pl.when(c - d >= 0)
+            def _():
+                project(i, c - d, False)
+
+            @pl.when(c + d < n)
+            def _():
+                project(i, c + d, False)
+
+    rows_out = out_ref.shape[0]
+
+    def rs_copy(d, sending):
+        r = lax.rem(t + d, tps) if sending else lax.rem(t + tps - d, tps)
+        return pltpu.make_async_remote_copy(
+            src_ref=part.at[d - 1], dst_ref=got.at[d - 1], send_sem=s_rs.at[d - 1], recv_sem=r_rs.at[d - 1],
+            device_id={"tp": r}, device_id_type=MESH)
+
+    for d in range(1, tps):
+        r = lax.rem(t + d, tps)
+        part[d - 1] = acc[pl.ds(al(r * rows_out, rows_out), rows_out), :].astype(BF16)
+        rs_copy(d, True).start()
+    total = acc[pl.ds(al(t * rows_out, rows_out), rows_out), :]
+    for d in range(1, tps):
+        rs_copy(d, False).wait_recv()
+        total = total + got[d - 1].astype(F32)
+    out_ref[...] = total.astype(BF16)
+
+    for i in range(nch):
+        for kind in kinds(i):
+            for d in range(1, n):
+                copy1(kind, i, d, True).wait_send()
+        for kind in (3, 4):
+            for e in range(1, groups):
+                for d in range(1, n):
+                    copy_y(kind, i, e, d, True).wait_send()
+        for b in range(n):
+            @pl.when(jnp.logical_and(b <= c, c + 1 < n))
+            def _():
+                ag_copy(i, b, True).wait_send()
+
+            @pl.when(jnp.logical_and(b >= c, c > 0))
+            def _():
+                ag_copy(i, b, False).wait_send()
+    for d in range(1, tps):
+        rs_copy(d, True).wait_send()
+
+
+def fast(sz, q_nope, q_rope, c_kv, k_rope, positions, w_uk, w_uv, w_out):
+    n, groups, tps, nch = sz["n"], sz["g"], sz["t"], sz["nch"]
+    tok, hpc, nope, rope, lat, vdim = (sz[k] for k in ("tok", "hpc", "nope", "rope", "lat", "vdim"))
+    hc = hpc // nch
+    seq = n * tok
+    cols = w_out.shape[1]
+    q_rot = rotate_flat(q_rope, positions, rope).astype(BF16)
+    k_rot = rotate(k_rope, positions).astype(BF16)
+    high = (positions // 256).astype(BF16)[:, None]
+    low = (positions % 256).astype(BF16)[:, None]
+    key_rows = jnp.concatenate([c_kv, k_rot, high, low, jnp.zeros((tok, rope - 2), BF16)], axis=1)
+    hbm = pl.BlockSpec(memory_space=pl.ANY)
+    dma = pltpu.SemaphoreType.DMA
+    return pl.pallas_call(
+        functools.partial(mega, sz),
+        out_shape=jax.ShapeDtypeStruct((seq // tps, cols), BF16),
+        in_specs=[hbm] * 6,
+        out_specs=pl.BlockSpec(memory_space=pltpu.VMEM),
+        scratch_shapes=[
+            pltpu.VMEM((seq, hpc * nope), BF16),
+            pltpu.VMEM((seq, hpc * rope), BF16),
+            pltpu.VMEM((seq, lat + 2 * rope), BF16),
+            pltpu.VMEM((hpc, nope, lat), BF16),
+            pltpu.VMEM((hpc, lat, vdim), BF16),
+            pltpu.VMEM(w_out.shape, BF16),
+            pltpu.VMEM((2, seq, 2 * rope), BF16),
+            pltpu.VMEM((n, nch, seq, hc * vdim), BF16),
+            pltpu.VMEM((seq, cols), F32),
+            pltpu.VMEM((tps - 1, seq // tps, cols), BF16),
+            pltpu.VMEM((tps - 1, seq // tps, cols), BF16),
+            dma((5, nch, n - 1)),
+            dma((5, nch, n - 1)),
+            dma((2, nch, max(groups - 1, 1), n - 1)),
+            dma((2, nch, max(groups - 1, 1), n - 1)),
+            dma((nch, n)),
+            dma((nch, n)),
+            dma((nch, n)),
+            dma((tps - 1,)),
+            dma((tps - 1,)),
+            dma((5, nch)),
+            dma,
+        ],
+        compiler_params=pltpu.CompilerParams(collective_id=0, has_side_effects=True,
+                                             vmem_limit_bytes=48 * 1024 * 1024),
+    )(q_nope, q_rot, key_rows, w_uk, w_uv, w_out)
+
+
+def general(q_nope, q_rope, c_kv, k_rope, positions, w_uk, w_uv, w_out):
     tok_count = q_nope.shape[0]
     head_count = w_uk.shape[0]
     latent = c_kv.shape[1]
@@ -69,6 +383,40 @@
         partial_value.astype(jnp.bfloat16), "tp", scatter_dimension=0, tiled=True
     )
     return summed
+
+
+CHUNKS = 2
+
+
+def on_device(sizes, *args):
+    q_nope, q_rope, c_kv, k_rope, positions, w_uk, w_uv, w_out = args
+    n, groups, tps = sizes["ctx"], sizes["groups"], sizes["tp"]
+    heads = w_uk.shape[0]
+    hpc = heads // n
+    sz = dict(n=n, g=groups, t=tps, nch=CHUNKS, tok=q_nope.shape[0], hpc=hpc,
+              nope=w_uk.shape[1] * n, rope=k_rope.shape[1], lat=c_kv.shape[1],
+              vdim=w_uv.shape[2], tile=256)
+    seq = n * sz["tok"]
+    cols = w_out.shape[1]
+    fits = (
+        heads % n == 0
+        and n > 1
+        and tps > 1
+        and hpc % (CHUNKS * groups) == 0
+        and (hpc // CHUNKS) % 2 == 0
+        and seq <= 512
+        and seq % (tps * 16) == 0
+        and sz["tok"] % 16 == 0
+        and sz["rope"] == 64
+        and sz["nope"] % 128 == 0
+        and sz["vdim"] % 128 == 0
+        and sz["lat"] % 128 == 0
+        and cols % 256 == 0
+        and w_out.size * 2 + seq * cols * 8 <= 32 * 2**20
+    )
+    if fits:
+        return fast(sz, *args)
+    return general(*args)
 
 
 def solution(mesh):
@@ -84,5 +432,6 @@
     )
     out_specs = P(("groups", "tp"), "ctx")
     return jax.shard_map(
-        on_device, mesh=mesh, in_specs=in_specs, out_specs=out_specs, check_vma=False
-    )
+        functools.partial(on_device, dict(mesh.shape)),
+        mesh=mesh, in_specs=in_specs, out_specs=out_specs, check_vma=False,
+    )

time: 269 us -> 110 us (0.41)
  waiting for transfers between devices: 201 us -> 0 us
  Pallas kernels: 0 us -> 98.3 us
  blocking collectives: 27.3 us -> 0 us
  matrix products: 20.4 us -> 0 us
  between operations: 13.9 us -> 0.08 us
  local copies, waits for them, and re-layouts: 4.14 us -> 8.4 us
    all_gather x3 -> x0, waiting for transfers between devices: 176 us -> none  [the longest x1 74 us: on_device(): lax.all_gather(w_uv, 'ctx', axis=1, tiled=True)]
    pallas_call x0 -> x1, Pallas kernels: none -> 98.3 us  [fast(): pl.pallas_call(functools.partial(mega, sz), out_shape=jax.ShapeDtypeStruc...]
    reduce_scatter x1 -> x0, waiting for transfers between devices: 22.9 us -> none  [on_device(): lax.psum_scatter(partial_value.astype(jnp.bfloat16), 'tp', scatter_dimens...]
    dot_general x5 -> x0, matrix products: 20.4 us -> none  [the longest x1 10.7 us: on_device(): jnp.dot(lax.all_gather(rows_out, 'ctx', axis=0, tiled=True), w_out, prefe...]
    all_gather x1 -> x0, blocking collectives: 17.4 us -> none  [on_device(): key_part = lax.all_gather(key_rows, 'ctx', axis=0, tiled=True)]
    unnamed x1 -> x0, blocking collectives: 9.92 us -> none
    unnamed x15 -> x7, local copies, waits for them, and re-layouts: 0.86 us -> 4.18 us
  transfers between devices with their start and end apart: 4 -> 0, of which waited for: 4 -> 0; matrix products, arithmetic and copies ran while one was open for 4% -> 0% of each run, Pallas kernels for 0% -> 0%
where the time goes in v1:
time: 110 us
  Pallas kernels  98.3 us (89%)
  local copies, waits for them, and re-layouts  8.4 us (8%)
  other arithmetic  2.92 us (3%)
    pallas_call x1, Pallas kernels, fast(): pl.pallas_call(functools.partial(mega, sz), out_shape=jax.ShapeDtypeStruc...  98.3 us
    unnamed x7, local copies, waits for them, and re-layouts  4.18 us

profile of v1, /device:TPU:0, one launch (start us, length us, event | category | flops | bytes accessed | tf_op | source)
XLA Modules:
  0.0 109.7 jit_solution(4219607423872560149)
XLA Ops:
  0.0 0.7 fusion.9
  0.8 1.0 fusion.7
  1.8 0.1 copy.18
  1.8 0.1 tile.8
  2.0 0.3 copy.19
  2.3 0.1 copy.20
  2.3 0.1 tile.20
  2.5 0.3 copy.21
  2.8 1.2 %fusion.11 = (f32[64,2016]{1,0:T(8,128)S(1)}, f32[64,2016]{1,0:T(8,128)S(1)}) fusion(bf16[64,2048]{1,0:T(8,128)(2,1)} %param.9), kind=kLoop, calls=%fused_computation.26 | loop fusion | bytes 2064384 | tf_op jit(solution)/shard_map/jit(_roll_static)/slice | solution.py:39
  4.0 0.8 fusion.10
  4.9 1.2 %fusion.3.qr_in = bf16[64,2048]{1,0:T(8,128)(2,1)S(1)} fusion(f32[64,2048]{1,0:T(8,128)S(1)} %copy.21, f32[64,32]{1,0:T(8,128)S(1)} %get-tuple-element.6, f32[64,2016]{1,0:T(8,128)S(1)} %get-tuple-element.8, f32[64,2016]{1,0:T(8,128)S(1)} %get-tuple-element.7, f32[64,32]{1,0:T(8,128)S(1)} %get-tuple-element.5, f32[64,2048]{1,0:T(8,128)S(1)} %copy.19, ...), kind=kLoop, calls=%fused_computation.4 | loop fusion | flops 1179648 | bytes 2623488 | tf_op jit(solution)/shard_map/convert_element_type | solution.py:294
  6.0 0.1 copy.22
  6.1 0.1 copy.23
  6.3 0.9 concatenate.16.kv_in
  7.2 0.0 copy-start
  7.2 1.2 %copy-done = bf16[32,32,512]{2,1,0:T(8,128)(2,1)S(1)} copy-done((bf16[32,32,512]{2,1,0:T(8,128)(2,1)S(1)}, bf16[32,32,512]{2,1,0:T(8,128)(2,1)}, u32[]{:S(2)}) %copy-start) | copy-done | bytes 1048600
  8.4 0.0 copy-start.1
  8.4 1.2 %copy-done.1 = bf16[32,128,128]{2,1,0:T(8,128)(2,1)S(1)} copy-done((bf16[32,128,128]{2,1,0:T(8,128)(2,1)S(1)}, bf16[32,128,128]{2,1,0:T(8,128)(2,1)}, u32[]{:S(2)}) %copy-start.1) | copy-done | bytes 1048600
  9.7 0.0 copy-start.2
  9.7 1.0 copy-done.2
  10.7 98.3 %shard_map.82 = bf16[64,1792]{1,0:T(8,128)(2,1)S(1)} custom-call(bf16[64,4096]{1,0:T(8,128)(2,1)S(1)} %copy-done.2, bf16[64,2048]{1,0:T(8,128)(2,1)S(1)} %fusion.3.qr_in, bf16[64,640]{1,0:T(8,128)(2,1)S(1)} %concatenate.16.kv_in, bf16[32,32,512]{2,1,0:T(8,128)(2,1)S(1)} %copy-done, bf16[32,128,128]{2,1,0:T(8,128)(2,1)S(1)} %copy-done.1, ...), custom_call_target="tpu_custom_call" | custom-call | tf_op jit(solution)/shard_map/pallas_call | solution.py:301
  109.0 0.7 copy.25
  (3 shorter events, 0.0 us)
Async XLA Ops:
  7.2 1.2 %copy-start = (bf16[32,32,512]{2,1,0:T(8,128)(2,1)S(1)}, bf16[32,32,512]{2,1,0:T(8,128)(2,1)}, u32[]{:S(2)}) copy-start(bf16[32,32,512]{2,1,0:T(8,128)(2,1)} %wuk_in.1) | copy-start | bytes 3145732
  8.4 1.2 %copy-start.1 = (bf16[32,128,128]{2,1,0:T(8,128)(2,1)S(1)}, bf16[32,128,128]{2,1,0:T(8,128)(2,1)}, u32[]{:S(2)}) copy-start(bf16[32,128,128]{2,1,0:T(8,128)(2,1)} %wuv_in.1) | copy-start | bytes 3145732
  9.7 1.0 copy-start.2

commit v2 on v1

--- a/solution.py
+++ b/solution.py
@@ -1,4 +1,5 @@
 import functools
+import math
 
 import jax
 import jax.numpy as jnp
@@ -26,23 +27,9 @@
     )
 
 
-def rotate_flat(values, position, rope_dim):
-    half_dim = rope_dim // 2
-    copies = values.shape[1] // half_dim
-    freqs = 10000.0 ** (-jnp.arange(half_dim, dtype=jnp.float32) / half_dim)
-    angles = position.astype(jnp.float32)[:, None] * freqs
-    cosine = jnp.tile(jnp.cos(angles), (1, copies))
-    sine = jnp.tile(jnp.sin(angles), (1, copies))
-    wide = values.astype(jnp.float32)
-    lane = lax.broadcasted_iota(jnp.int32, wide.shape, 1)
-    low = lax.rem(lane, rope_dim) < half_dim
-    other = jnp.where(low, -jnp.roll(wide, -half_dim, axis=1), jnp.roll(wide, half_dim, axis=1))
-    return wide * cosine + other * sine
-
-
-def mega(sz, qn_in, qr_in, kv_in, wuk_in, wuv_in, wout_in, out_ref,
-         qn, qr, kv, wuk, wuv, wout, krot, ho, acc, part, got,
-         s1, r1, sy, ry, s_right, s_left, r_ag, s_rs, r_rs, loc, loc_out):
+def mega(sz, qn_in, qr_in, kv_in, kr_in, pos_in, wuk_in, wuv_in, wout_in, out_ref,
+         qn, qr, kv, kr, pos, wuk, wuv, wout, krot, table, limit, ho, acc, part, got,
+         s1, r1, sy, ry, st, rt, s_right, s_left, r_ag, s_rs, r_rs, loc, loc_out):
     n, groups, tps, nch = sz["n"], sz["g"], sz["t"], sz["nch"]
     tok, hpc, nope, rope, lat, vdim = (sz[k] for k in ("tok", "hpc", "nope", "rope", "lat", "vdim"))
     scale = (nope + rope) ** (-0.5)
@@ -53,6 +40,7 @@
     t = lax.axis_index("tp")
     nsl = nope // n
     lsl = lat // n
+    share = tok // tps
 
     barrier = pltpu.get_barrier_semaphore()
     for axis, me, count in (("ctx", c, n), ("groups", g, groups), ("tp", t, tps)):
@@ -63,14 +51,18 @@
     def al(x, m):
         return pl.multiple_of(x, m)
 
-    my_rows = pl.ds(al(c * tok, tok), tok)
-
     def rows_of(s):
         return pl.ds(al(s * tok, tok), tok)
 
-    def piece(kind, i, j, s, gg):
-        if kind == 0:
-            return kv_in, kv.at[rows_of(s), :]
+    def piece(kind, i, j, s, part_of):
+        if kind in (0, 5):
+            src, dst = (kv_in, kv) if kind == 0 else (kr_in, kr)
+            if part_of is None:
+                return src, dst.at[rows_of(s), :]
+            return (src.at[pl.ds(al(part_of * share, share), share), :],
+                    dst.at[pl.ds(al(s * tok + part_of * share, share), share), :])
+        if kind == 6:
+            return pos_in, pos.at[s]
         if kind == 1:
             w = hc * nope
             return (qn_in.at[:, pl.ds(al(j * (hpc * nope) + i * w, w), w)],
@@ -79,21 +71,23 @@
             w = hc * rope
             return (qr_in.at[:, pl.ds(al(j * (hpc * rope) + i * w, w), w)],
                     qr.at[rows_of(s), pl.ds(i * w, w)])
-        if gg is None:
+        if part_of is None:
             src_h, dst_h = pl.ds(j * hpc + i * hc, hc), pl.ds(i * hc, hc)
         else:
-            src_h, dst_h = pl.ds(j * hpc + i * hc + gg * hg, hg), pl.ds(i * hc + gg * hg, hg)
+            src_h = pl.ds(j * hpc + i * hc + part_of * hg, hg)
+            dst_h = pl.ds(i * hc + part_of * hg, hg)
         if kind == 3:
             return wuk_in.at[src_h], wuk.at[dst_h, pl.ds(al(s * nsl, nsl), nsl), :]
         return wuv_in.at[src_h], wuv.at[dst_h, pl.ds(al(s * lsl, lsl), lsl), :]
 
     def copy1(kind, i, d, sending):
+        mine = t if kind in (0, 5) else g
         if sending:
             j = lax.rem(c + d, n)
-            src, dst = piece(kind, i, j, c, g)
+            src, dst = piece(kind, i, j, c, mine)
         else:
             j = lax.rem(c + n - d, n)
-            src, dst = piece(kind, i, c, j, g)
+            src, dst = piece(kind, i, c, j, mine)
         return pltpu.make_async_remote_copy(
             src_ref=src, dst_ref=dst, send_sem=s1.at[kind, i, d - 1], recv_sem=r1.at[kind, i, d - 1],
             device_id={"ctx": j}, device_id_type=MESH)
@@ -103,13 +97,17 @@
         return pltpu.make_async_copy(src, dst, loc.at[kind, i])
 
     def kinds(i):
-        return (0, 1, 2, 3, 4) if i == 0 else (1, 2, 3, 4)
-
+        return (0, 1, 2, 3, 4, 5, 6) if i == 0 else (1, 2, 3, 4)
+
+    order = [((6, 0, 5), 0), ((3, 4), 0)]
     for i in range(nch):
-        for kind in (3, 4, 0, 1, 2):
-            if kind in kinds(i):
-                for d in range(n - 1, 0, -1):
-                    copy1(kind, i, d, True).start()
+        if i + 1 < nch:
+            order.append(((3, 4), i + 1))
+        order.append(((1, 2), i))
+    for group, i in order:
+        for kind in group:
+            for d in range(n - 1, 0, -1):
+                copy1(kind, i, d, True).start()
     for i in range(nch):
         for kind in kinds(i):
             local(kind, i).start()
@@ -126,6 +124,16 @@
             recv_sem=ry.at[kind - 3, i, e - 1, d - 1],
             device_id={"groups": to}, device_id_type=MESH)
 
+    def copy_t(kind, e, d, sending):
+        s = lax.rem(c + n - d, n)
+        owner = t if sending else lax.rem(t + tps - e, tps)
+        _, dst = piece(kind, 0, c, s, owner)
+        to = lax.rem(t + e, tps) if sending else owner
+        return pltpu.make_async_remote_copy(
+            src_ref=dst, dst_ref=dst, send_sem=st.at[kind // 5, e - 1, d - 1],
+            recv_sem=rt.at[kind // 5, e - 1, d - 1],
+            device_id={"tp": to}, device_id_type=MESH)
+
     def forward_weights(i):
         for kind in (3, 4):
             for d in range(1, n):
@@ -133,42 +141,72 @@
                 for e in range(1, groups):
                     copy_y(kind, i, e, d, True).start()
 
-    def ag_ref(i, b):
-        return ho.at[b, i]
+    def forward_keys():
+        for d in range(1, n):
+            for kind in (0, 5):
+                copy1(kind, 0, d, False).wait_recv()
+                for e in range(1, tps):
+                    copy_t(kind, e, d, True).start()
 
     def ag_copy(i, b, right):
-        ref = ag_ref(i, b)
+        ref = ho.at[b, i]
         return pltpu.make_async_remote_copy(
             src_ref=ref, dst_ref=ref, send_sem=(s_right if right else s_left).at[i, b],
             recv_sem=r_ag.at[i, b],
             device_id={"ctx": c + 1 if right else c - 1}, device_id_type=MESH)
 
+    wide = 2 * rope
+
+    def turn(x):
+        lane = lax.broadcasted_iota(jnp.int32, x.shape, 1)
+        low = lax.rem(lane, rope) < rope // 2
+        other = jnp.where(low, -pltpu.roll(x, wide - rope // 2, 1), pltpu.roll(x, rope // 2, 1))
+        return x * table[0] + other * table[1]
+
+    def tables():
+        seq = n * tok
+        for d in range(1, n):
+            copy1(6, 0, d, False).wait_recv()
+        local(6, 0).wait()
+        row = jnp.concatenate([pos[s] for s in range(n)], axis=1).astype(F32)
+        col = jnp.broadcast_to(row, (wide, seq)).T
+        lane = lax.broadcasted_iota(jnp.int32, (1, wide), 1)
+        index = lax.rem(lane, rope // 2).astype(F32)
+        freqs = jnp.exp(index * (-math.log(10000.0) / (rope // 2)))
+        angles = col * freqs
+        table[0] = jnp.cos(angles)
+        table[1] = jnp.sin(angles)
+        limit[...] = jnp.where(row > col[:, :1], -1e30, 3e38)
+
+    def keys():
+        for kind in (0, 5):
+            local(kind, 0).wait()
+            for e in range(1, tps):
+                for d in range(1, n):
+                    copy_t(kind, e, d, False).wait_recv()
+        raw = kr[...].astype(F32)
+        turned = turn(jnp.concatenate([raw, raw], axis=1))
+        lane = lax.broadcasted_iota(jnp.int32, turned.shape, 1)
+        krot[0] = jnp.where(lane < rope, turned, 0.0).astype(BF16)
+        krot[1] = jnp.where(lane < rope, 0.0, turned).astype(BF16)
+
     def attend(i):
-        blk = kv[:, lat:lat + 2 * rope].astype(F32)
-        lane = lax.broadcasted_iota(jnp.int32, blk.shape, 1)
-        pos_col = jnp.sum(jnp.where(lane == rope, blk * 256.0, jnp.where(lane == rope + 1, blk, 0.0)),
-                          axis=1, keepdims=True)
-        blk_t = blk.T
-        pos_row = blk_t[rope:rope + 1, :] * 256.0 + blk_t[rope + 1:rope + 2, :]
-        hidden = pos_row > pos_col
-        even = jnp.where(lane < rope, blk, 0.0)
-        krot[0] = even.astype(BF16)
-        krot[1] = pltpu.roll(even, rope, 1).astype(BF16)
         nt = (((1,), (1,)), ((), ()))
 
         def pair(p, carry):
-            qrp = qr[:, pl.ds(al((i * (hc // 2) + p) * 2 * rope, 2 * rope), 2 * rope)]
+            raw = qr[:, pl.ds(al((i * (hc // 2) + p) * wide, wide), wide)]
+            qrp = turn(raw.astype(F32)).astype(BF16)
             for k in range(2):
                 hl = 2 * p + k
                 h = i * hc + hl
                 q = qn[:, pl.ds(al(h * nope, nope), nope)]
                 ql = jnp.dot(q, wuk[h], preferred_element_type=F32).astype(BF16)
-                sc = lax.dot_general(ql, kv[:, :lat], nt, preferred_element_type=F32)
+                sc = lax.dot_general(ql, kv[...], nt, preferred_element_type=F32)
                 sc = (sc + lax.dot_general(qrp, krot[k], nt, preferred_element_type=F32)) * scale
-                sc = jnp.where(hidden, -1e30, sc)
+                sc = jnp.minimum(sc, limit[...])
                 w = jnp.exp(sc - jnp.max(sc, axis=1, keepdims=True))
                 total = jnp.sum(w, axis=1, keepdims=True)
-                o = jnp.dot(w.astype(BF16), kv[:, :lat], preferred_element_type=F32)
+                o = jnp.dot(w.astype(BF16), kv[...], preferred_element_type=F32)
                 o = (o / total).astype(BF16)
                 ho[c, i, :, pl.ds(al(hl * vdim, vdim), vdim)] = jnp.dot(
                     o, wuv[h], preferred_element_type=F32).astype(BF16)
@@ -176,21 +214,22 @@
 
         lax.fori_loop(0, hc // 2, pair, 0)
 
+    forward_keys()
+    forward_weights(0)
+    tables()
+    keys()
     for i in range(nch):
-        if i == 0:
-            forward_weights(0)
-        for kind in (0, 1, 2):
-            if kind in kinds(i):
-                for d in range(1, n):
-                    copy1(kind, i, d, False).wait_recv()
-        for kind in kinds(i):
+        if i + 1 < nch:
+            forward_weights(i + 1)
+        for kind in (1, 2):
+            for d in range(1, n):
+                copy1(kind, i, d, False).wait_recv()
+        for kind in (1, 2, 3, 4):
             local(kind, i).wait()
         for kind in (3, 4):
             for e in range(1, groups):
                 for d in range(1, n):
                     copy_y(kind, i, e, d, False).wait_recv()
-        if i + 1 < nch:
-            forward_weights(i + 1)
         attend(i)
 
         @pl.when(c + 1 < n)
@@ -281,6 +320,10 @@
             @pl.when(jnp.logical_and(b >= c, c > 0))
             def _():
                 ag_copy(i, b, False).wait_send()
+    for kind in (0, 5):
+        for e in range(1, tps):
+            for d in range(1, n):
+                copy_t(kind, e, d, True).wait_send()
     for d in range(1, tps):
         rs_copy(d, True).wait_send()
 
@@ -291,45 +334,47 @@
     hc = hpc // nch
     seq = n * tok
     cols = w_out.shape[1]
-    q_rot = rotate_flat(q_rope, positions, rope).astype(BF16)
-    k_rot = rotate(k_rope, positions).astype(BF16)
-    high = (positions // 256).astype(BF16)[:, None]
-    low = (positions % 256).astype(BF16)[:, None]
-    key_rows = jnp.concatenate([c_kv, k_rot, high, low, jnp.zeros((tok, rope - 2), BF16)], axis=1)
-    hbm = pl.BlockSpec(memory_space=pl.ANY)
+    hbm = pl.BlockSpec(memory_space=pltpu.HBM)
     dma = pltpu.SemaphoreType.DMA
+    more = max(groups - 1, 1)
     return pl.pallas_call(
         functools.partial(mega, sz),
         out_shape=jax.ShapeDtypeStruct((seq // tps, cols), BF16),
-        in_specs=[hbm] * 6,
+        in_specs=[hbm] * 8,
         out_specs=pl.BlockSpec(memory_space=pltpu.VMEM),
         scratch_shapes=[
             pltpu.VMEM((seq, hpc * nope), BF16),
             pltpu.VMEM((seq, hpc * rope), BF16),
-            pltpu.VMEM((seq, lat + 2 * rope), BF16),
+            pltpu.VMEM((seq, lat), BF16),
+            pltpu.VMEM((seq, rope), BF16),
+            pltpu.VMEM((n, 1, tok), jnp.int32),
             pltpu.VMEM((hpc, nope, lat), BF16),
             pltpu.VMEM((hpc, lat, vdim), BF16),
             pltpu.VMEM(w_out.shape, BF16),
             pltpu.VMEM((2, seq, 2 * rope), BF16),
+            pltpu.VMEM((2, seq, 2 * rope), F32),
+            pltpu.VMEM((seq, seq), F32),
             pltpu.VMEM((n, nch, seq, hc * vdim), BF16),
             pltpu.VMEM((seq, cols), F32),
             pltpu.VMEM((tps - 1, seq // tps, cols), BF16),
             pltpu.VMEM((tps - 1, seq // tps, cols), BF16),
-            dma((5, nch, n - 1)),
-            dma((5, nch, n - 1)),
-            dma((2, nch, max(groups - 1, 1), n - 1)),
-            dma((2, nch, max(groups - 1, 1), n - 1)),
+            dma((7, nch, n - 1)),
+            dma((7, nch, n - 1)),
+            dma((2, nch, more, n - 1)),
+            dma((2, nch, more, n - 1)),
+            dma((2, tps - 1, n - 1)),
+            dma((2, tps - 1, n - 1)),
             dma((nch, n)),
             dma((nch, n)),
             dma((nch, n)),
             dma((tps - 1,)),
             dma((tps - 1,)),
-            dma((5, nch)),
+            dma((7, nch)),
             dma,
         ],
         compiler_params=pltpu.CompilerParams(collective_id=0, has_side_effects=True,
-                                             vmem_limit_bytes=48 * 1024 * 1024),
-    )(q_nope, q_rot, key_rows, w_uk, w_uv, w_out)
+                                             vmem_limit_bytes=60 * 1024 * 1024),
+    )(q_nope, q_rope, c_kv, k_rope, positions.reshape(1, tok), w_uk, w_uv, w_out)
 
 
 def general(q_nope, q_rope, c_kv, k_rope, positions, w_uk, w_uv, w_out):
@@ -385,7 +430,7 @@
     return summed
 
 
-CHUNKS = 2
+CHUNKS = 4
 
 
 def on_device(sizes, *args):
@@ -406,7 +451,7 @@
         and (hpc // CHUNKS) % 2 == 0
         and seq <= 512
         and seq % (tps * 16) == 0
-        and sz["tok"] % 16 == 0
+        and sz["tok"] % (tps * 16) == 0
         and sz["rope"] == 64
         and sz["nope"] % 128 == 0
         and sz["vdim"] % 128 == 0

time: 110 us -> 95.4 us (0.87)
  local copies, waits for them, and re-layouts: 8.4 us -> 1.64 us
  Pallas kernels: 98.3 us -> 92.6 us
  other arithmetic: 2.92 us -> 0 us
    pallas_call x1, Pallas kernels: 98.3 us -> 92.6 us  [fast(): pl.pallas_call(functools.partial(mega, sz), out_shape=jax.ShapeDtypeStruc...]
    unnamed x7 -> x1, local copies, waits for them, and re-layouts: 4.18 us -> 1.64 us
    slice x2 -> x0, local copies, waits for them, and re-layouts: 2.03 us -> none  [rotate_flat(): jnp.roll(wide, half_dim, axis=1)]
    convert_element_type x1 -> x0, other arithmetic: 1.17 us -> none  [fast(): q_rot = rotate_flat(q_rope, positions, rope).astype(BF16)]
where the time goes in v2:
time: 95.4 us; the launch traced here: 94.2 us
  Pallas kernels  92.6 us (97%)
  local copies, waits for them, and re-layouts  1.64 us (2%)
    pallas_call x1, Pallas kernels, fast(): pl.pallas_call(functools.partial(mega, sz), out_shape=jax.ShapeDtypeStruc...  92.6 us

profile of v2, /device:TPU:0, one launch (start us, length us, event | category | flops | bytes accessed | tf_op | source)
XLA Modules:
  0.0 94.2 jit_solution(13326597003361211669)
XLA Ops:
  0.0 92.6 %shard_map.82 = bf16[64,1792]{1,0:T(8,128)(2,1)} custom-call(bf16[64,4096]{1,0:T(8,128)(2,1)} %qn_in.1, bf16[64,2048]{1,0:T(8,128)(2,1)} %qr_in.1, bf16[64,512]{1,0:T(8,128)(2,1)} %kv_in.1, bf16[64,64]{1,0:T(8,128)(2,1)} %kr_in.1, s32[1,64]{1,0:T(1,128)} %bitcast.1, bf16[32,32,512]{2,1,0:T(8,128)(2,1)} %wuk_in.1, bf16[32,128,128]{2,1,0:T(8,128)(2,1)} %wuv_in.1, ...), custom_call_target="tpu_custom_call" | custom-call | tf_op jit(solution)/shard_map/pallas_call | solution.py:340
  92.6 1.6 %copy.10 = bf16[64,1792]{1,0:T(8,128)(2,1)} copy(bf16[64,1792]{1,0:T(8,128)(2,1)} %shard_map.82) | data formatting | bytes 458752

commit v3 on v2

--- a/solution.py
+++ b/solution.py
@@ -255,11 +255,18 @@
 
         lax.fori_loop(0, cols // tile, step, 0)
 
-    wout_copy.wait()
-    for i in range(nch):
-        project(i, c, i == 0)
+    waited = False
     for d in range(1, n):
         for i in range(nch):
+            @pl.when(c + d < n)
+            def _():
+                b = c + d
+                ag_copy(i, b, False).wait_recv()
+
+                @pl.when(c > 0)
+                def _():
+                    ag_copy(i, b, False).start()
+
             @pl.when(c - d >= 0)
             def _():
                 b = c - d
@@ -269,14 +276,11 @@
                 def _():
                     ag_copy(i, b, True).start()
 
-            @pl.when(c + d < n)
-            def _():
-                b = c + d
-                ag_copy(i, b, False).wait_recv()
-
-                @pl.when(c > 0)
-                def _():
-                    ag_copy(i, b, False).start()
+            if not waited:
+                wout_copy.wait()
+                waited = True
+            if d == 1:
+                project(i, c, i == 0)
 
             @pl.when(c - d >= 0)
             def _():
@@ -287,22 +291,36 @@
                 project(i, c + d, False)
 
     rows_out = out_ref.shape[0]
-
-    def rs_copy(d, sending):
-        r = lax.rem(t + d, tps) if sending else lax.rem(t + tps - d, tps)
+    half = cols // 2
+    core = lax.rem(t, 2)
+    mate = t + 1 - 2 * core
+    across = lax.rem(t + 2, tps)
+    mate_across = lax.rem(mate + 2, tps)
+
+    def block(r, at):
+        return acc[pl.ds(al(r * rows_out, rows_out), rows_out), at]
+
+    def rs_copy(stage, k):
+        at = pl.ds(k * half, half)
+        blocks = pl.ds(0, 2) if stage == 0 else pl.ds(2, 1)
         return pltpu.make_async_remote_copy(
-            src_ref=part.at[d - 1], dst_ref=got.at[d - 1], send_sem=s_rs.at[d - 1], recv_sem=r_rs.at[d - 1],
-            device_id={"tp": r}, device_id_type=MESH)
-
-    for d in range(1, tps):
-        r = lax.rem(t + d, tps)
-        part[d - 1] = acc[pl.ds(al(r * rows_out, rows_out), rows_out), :].astype(BF16)
-        rs_copy(d, True).start()
-    total = acc[pl.ds(al(t * rows_out, rows_out), rows_out), :]
-    for d in range(1, tps):
-        rs_copy(d, False).wait_recv()
-        total = total + got[d - 1].astype(F32)
-    out_ref[...] = total.astype(BF16)
+            src_ref=part.at[blocks, :, at], dst_ref=got.at[blocks, :, at],
+            send_sem=s_rs.at[stage, k], recv_sem=r_rs.at[stage, k],
+            device_id={"tp": mate if stage == 0 else across}, device_id_type=MESH)
+
+    spans = [slice(k * half, (k + 1) * half) for k in range(2)]
+    for k, at in enumerate(spans):
+        part[1, :, at] = block(mate_across, at).astype(BF16)
+        part[0, :, at] = block(mate, at).astype(BF16)
+        rs_copy(0, k).start()
+    for k, at in enumerate(spans):
+        rs_copy(0, k).wait_recv()
+        part[2, :, at] = (block(across, at) + got[1, :, at].astype(F32)).astype(BF16)
+        rs_copy(1, k).start()
+    for k, at in enumerate(spans):
+        own = block(t, at) + got[0, :, at].astype(F32)
+        rs_copy(1, k).wait_recv()
+        out_ref[:, at] = (own + got[2, :, at].astype(F32)).astype(BF16)
 
     for i in range(nch):
         for kind in kinds(i):
@@ -324,8 +342,9 @@
         for e in range(1, tps):
             for d in range(1, n):
                 copy_t(kind, e, d, True).wait_send()
-    for d in range(1, tps):
-        rs_copy(d, True).wait_send()
+    for k in range(2):
+        rs_copy(0, k).wait_send()
+        rs_copy(1, k).wait_send()
 
 
 def fast(sz, q_nope, q_rope, c_kv, k_rope, positions, w_uk, w_uv, w_out):
@@ -367,8 +386,8 @@
             dma((nch, n)),
             dma((nch, n)),
             dma((nch, n)),
-            dma((tps - 1,)),
-            dma((tps - 1,)),
+            dma((2, 2)),
+            dma((2, 2)),
             dma((7, nch)),
             dma,
         ],
@@ -440,13 +459,13 @@
     hpc = heads // n
     sz = dict(n=n, g=groups, t=tps, nch=CHUNKS, tok=q_nope.shape[0], hpc=hpc,
               nope=w_uk.shape[1] * n, rope=k_rope.shape[1], lat=c_kv.shape[1],
-              vdim=w_uv.shape[2], tile=256)
+              vdim=w_uv.shape[2], tile=w_out.shape[1] // 2)
     seq = n * sz["tok"]
     cols = w_out.shape[1]
     fits = (
         heads % n == 0
         and n > 1
-        and tps > 1
+        and tps == 4
         and hpc % (CHUNKS * groups) == 0
         and (hpc // CHUNKS) % 2 == 0
         and seq <= 512

time: 95.4 us -> 89.4 us (0.937)
  Pallas kernels: 92.6 us -> 87.5 us
    pallas_call x1, Pallas kernels: 92.6 us -> 87.5 us  [fast(): pl.pallas_call(functools.partial(mega, sz), out_shape=jax.ShapeDtypeStruc...]
where the time goes in v3:
time: 89.4 us; the launch traced here: 89.1 us
  Pallas kernels  87.5 us (98%)
  local copies, waits for them, and re-layouts  1.64 us (2%)
    pallas_call x1, Pallas kernels, fast(): pl.pallas_call(functools.partial(mega, sz), out_shape=jax.ShapeDtypeStruc...  87.5 us

profile of v3, /device:TPU:0, one launch (start us, length us, event | category | flops | bytes accessed | tf_op | source)
XLA Modules:
  0.0 89.1 jit_solution(9837944331803187483)
XLA Ops:
  0.0 87.5 %shard_map.82 = bf16[64,1792]{1,0:T(8,128)(2,1)} custom-call(bf16[64,4096]{1,0:T(8,128)(2,1)} %qn_in.1, bf16[64,2048]{1,0:T(8,128)(2,1)} %qr_in.1, bf16[64,512]{1,0:T(8,128)(2,1)} %kv_in.1, bf16[64,64]{1,0:T(8,128)(2,1)} %kr_in.1, s32[1,64]{1,0:T(1,128)} %bitcast.1, bf16[32,32,512]{2,1,0:T(8,128)(2,1)} %wuk_in.1, bf16[32,128,128]{2,1,0:T(8,128)(2,1)} %wuv_in.1, ...), custom_call_target="tpu_custom_call" | custom-call | tf_op jit(solution)/shard_map/pallas_call | solution.py:359
  87.5 1.6 %copy.10 = bf16[64,1792]{1,0:T(8,128)(2,1)} copy(bf16[64,1792]{1,0:T(8,128)(2,1)} %shard_map.82) | data formatting | bytes 458752
